TPU v7x, 32 devices: a whole 2x2x4 slice. The times are simulated.
32 devices in a mesh: dap: 8 (over z, x), cplx: 4 (over y, core).
Axes of the slice: x: 2, y: 2, z: 4, core: 2. Of those that a mesh axis runs over, the one named last changes fastest.
Arguments:
- pair: bfloat16 [96, 384, 128], P('dap', 'cplx'), parts along dimension 1, may hold values from -6 to 6
- cotangent: bfloat16 [96, 384, 128], P('dap', 'cplx'), parts along dimension 1, may hold values from -6 to 6
- residue_mask: int32 [384], P('cplx'), parts along dimension 0, may hold values 0 or 1
- chain_ids: int32 [384], P('cplx'), parts along dimension 0, may hold values from 0 to 2, never falling along the last dimension, each value on 1 to 48 neighbouring positions
- chain_embed: float32 [2, 128], replicated, may hold values from -4 to 4
- out_norm_gain: float32 [128], replicated, may hold values from 0.25 to 1.75
- out_proj: bfloat16 [128, 512], replicated, may hold values from -0.5 to 0.5
- out_gate: bfloat16 [128, 128], replicated, may hold values from -0.5 to 0.5
- out_mid_gain: float32 [128], replicated, may hold values from 0.25 to 1.75
- out_final: bfloat16 [128, 128], replicated, may hold values from -0.5 to 0.5
- in_norm_gain: float32 [128], replicated, may hold values from 0.25 to 1.75
- in_proj: bfloat16 [128, 512], replicated, may hold values from -0.5 to 0.5
- in_gate: bfloat16 [128, 128], replicated, may hold values from -0.5 to 0.5
- in_mid_gain: float32 [128], replicated, may hold values from 0.25 to 1.75
- in_final: bfloat16 [128, 128], replicated, may hold values from -0.5 to 0.5
Outputs:
- pair_grad: bfloat16 [96, 384, 128], P('dap', 'cplx'), parts along dimension 1
- grad_proj: float32 [512, 512], P('cplx'), parts along dimension 0
- grad_gate: float32 [512, 128], P('cplx'), parts along dimension 0
- grad_final: float32 [512, 128], P('cplx'), parts along dimension 0
- grad_norm_gain: float32 [512], P('cplx'), parts along dimension 0
- grad_mid_gain: float32 [512], P('cplx'), parts along dimension 0
There are 4 independent parts, one for each index of `cplx`. A program takes and returns all parts, laid end to end along the dimension named above; an argument that names none is the same for every part. Nothing has to cross between parts.
Inputs may be any that keep to these rules, and one draw needn't show every extreme that they name: `chain_ids`: chain numbers never fall along the residues; each chain has at most 48 residues.
All inputs are finite; a program needn't handle non-finite values.
Results may differ from a plain program's by a relative error of at most 0.019.
Values may be sent and summed in bfloat16 or wider, within the bound.
A program may use at most 128 MiB of HBM per device.

v0:
```python
import jax
import jax.numpy as jnp
from jax import lax
from jax.sharding import PartitionSpec as P


def layer_norm(values_in, gain):
    average = jnp.mean(values_in, axis=-1, keepdims=True)
    centred = values_in - average
    variance = jnp.mean(centred * centred, axis=-1, keepdims=True)
    return centred * lax.rsqrt(variance + 1e-05) * gain


def gated_pair(projected, pair_mask, hidden_width):
    masked = pair_mask[..., None]
    left_act = (
        masked
        * jax.nn.sigmoid(projected[..., :hidden_width])
        * projected[..., hidden_width : 2 * hidden_width]
    )
    right_act = (
        masked
        * jax.nn.sigmoid(projected[..., 2 * hidden_width : 3 * hidden_width])
        * projected[..., 3 * hidden_width :]
    )
    return (left_act, right_act)


def shards(
    pair,
    cotangent,
    residue_mask,
    chain_ids,
    chain_embed,
    out_norm_gain,
    out_proj,
    out_gate,
    out_mid_gain,
    out_final,
    in_norm_gain,
    in_proj,
    in_gate,
    in_mid_gain,
    in_final,
):
    f32 = jnp.float32
    bf16 = jnp.bfloat16
    row_count = pair.shape[0]
    res_count = pair.shape[1]
    hidden_width = out_final.shape[0]
    inv_count = 1.0 / res_count
    row_start = lax.axis_index("dap") * row_count
    row_mask = lax.dynamic_slice_in_dim(residue_mask, row_start, row_count, 0)
    row_chain = lax.dynamic_slice_in_dim(chain_ids, row_start, row_count, 0)
    pair_mask = (row_mask[:, None] * residue_mask[None, :]).astype(f32)
    same_chain = row_chain[:, None] == chain_ids[None, :]
    start = pair.astype(f32) + jnp.where(same_chain[..., None], chain_embed[1], chain_embed[0])
    out_normed = layer_norm(start, out_norm_gain).astype(bf16)
    projected = jnp.dot(out_normed, out_proj, preferred_element_type=f32)
    left_act, right_act = gated_pair(projected, pair_mask, hidden_width)
    left_b = left_act.astype(bf16)
    right_b = right_act.astype(bf16)
    x_out = jnp.einsum(
        "ikc,jkc->ijc",
        left_b,
        lax.all_gather(right_b, "dap", axis=0, tiled=True),
        preferred_element_type=f32,
    )
    y_out = layer_norm(x_out, out_mid_gain).astype(bf16)
    update = jax.nn.sigmoid(jnp.dot(out_normed, out_gate, preferred_element_type=f32)) * jnp.dot(
        y_out, out_final, preferred_element_type=f32
    )
    pair_mid = (start + update).astype(bf16)
    mid_f32 = pair_mid.astype(f32)
    normed_f32, norm_back = jax.vjp(layer_norm, mid_f32, in_norm_gain)
    in_normed = normed_f32.astype(bf16)
    proj_in = jnp.dot(in_normed, in_proj, preferred_element_type=f32)
    (left_in, right_in), glu_back = jax.vjp(
        lambda proj_val: gated_pair(proj_val, pair_mask, hidden_width), proj_in
    )
    left_ib = left_in.astype(bf16)
    right_ib = right_in.astype(bf16)
    columns = lax.all_to_all(left_ib, "dap", split_axis=1, concat_axis=0, tiled=True)
    left_block = columns
    x_in = jnp.einsum(
        "kic,kjc->ijc",
        left_block,
        lax.all_gather(right_ib, "dap", axis=0, tiled=True),
        preferred_element_type=f32,
    )
    y_f32, mid_back = jax.vjp(layer_norm, x_in, in_mid_gain)
    y_in = y_f32.astype(bf16)
    logit = jnp.dot(in_normed, in_gate, preferred_element_type=f32)
    value = jnp.dot(y_in, in_final, preferred_element_type=f32)
    sigma = jax.nn.sigmoid(logit)
    upstream = cotangent.astype(f32)
    grad_value = (upstream * sigma).astype(bf16)
    grad_logit = (upstream * value * sigma * (1.0 - sigma)).astype(bf16)
    grad_final = jnp.einsum("ijc,ijd->cd", y_in, grad_value, preferred_element_type=f32) * inv_count
    grad_gate = (
        jnp.einsum("ijc,ijd->cd", in_normed, grad_logit, preferred_element_type=f32) * inv_count
    )
    grad_y = jnp.dot(grad_value, in_final.T, preferred_element_type=f32)
    grad_x, grad_mid = mid_back(grad_y)
    grad_x_b = grad_x.astype(bf16)
    shard_rows = lax.all_gather(grad_x_b, "dap", axis=0, tiled=True)
    left_block = left_ib
    grad_right = jnp.einsum("kic,ijc->kjc", left_block, shard_rows, preferred_element_type=f32)
    new_block = jnp.einsum("kjc,ijc->kic", right_ib, shard_rows, preferred_element_type=f32)
    grad_p = glu_back((new_block, grad_right))[0].astype(bf16)
    grad_proj = jnp.einsum("ijc,ijd->cd", in_normed, grad_p, preferred_element_type=f32) * inv_count
    grad_normed = jnp.dot(grad_p, in_proj.T, preferred_element_type=f32) + jnp.dot(
        grad_logit, in_gate.T, preferred_element_type=f32
    )
    grad_z, grad_norm = norm_back(grad_normed)
    pair_grad = (upstream + grad_z).astype(bf16)
    reduced = (
        lax.psum(grad_proj.astype(jnp.bfloat16), "dap").astype(jnp.float32),
        lax.psum(grad_gate.astype(jnp.bfloat16), "dap").astype(jnp.float32),
        lax.psum(grad_final.astype(jnp.bfloat16), "dap").astype(jnp.float32),
        lax.psum((grad_norm * inv_count).astype(jnp.bfloat16), "dap").astype(jnp.float32),
        lax.psum((grad_mid * inv_count).astype(jnp.bfloat16), "dap").astype(jnp.float32),
    )
    return (pair_grad, reduced[0], reduced[1], reduced[2], reduced[3], reduced[4])


def solution(mesh):
    placed = (
        P("dap", "cplx", None),
        P("dap", "cplx", None),
        P("cplx"),
        P("cplx"),
        P(),
        P(),
        P(),
        P(),
        P(),
        P(),
        P(),
        P(),
        P(),
        P(),
        P(),
    )
    return jax.shard_map(
        shards,
        mesh=mesh,
        in_specs=placed,
        out_specs=(
            P("dap", "cplx", None),
            P("cplx", None),
            P("cplx", None),
            P("cplx", None),
            P("cplx"),
            P("cplx"),
        ),
        check_vma=False,
    )
```

profile of v0, /device:TPU:0, one launch (start us, length us, event | category | flops | bytes accessed | tf_op | source)
XLA Modules:
  0.0 371.3 jit_solution(1143531026395006253)
XLA Ops:
  9.5 1.4 fusion.41
  10.9 1.6 multiply_reduce_fusion.7
  13.9 1.9 fusion.47
  17.0 1.2 copy.47
  18.3 1.7 fusion.8
  19.9 51.8 %all-gather.4.cloned.1.call-done = bf16[96,96,128]{2,1,0:T(8,128)(2,1)} async-done(((bf16[12,96,128]{2,1,0:T(8,128)(2,1)}), bf16[96,96,128]{2,1,0:T(8,128)(2,1)}) %all-gather.4.cloned.1.call-update) | async-done | bytes 2359312 | tf_op jit(solution)/shard_map/all_gather | solution.py:66
  71.7 3.5 copy.46
  75.2 2.8 fusion.62
  81.5 1.4 copy-done.1
  84.9 3.5 all-to-all-start
  89.5 17.3 %all-to-all-done = bf16[12,96,128]{2,0,1:T(8,128)(2,1)S(1)} async-done(((bf16[12,96,128]{2,0,1:T(8,128)(2,1)}), bf16[12,96,128]{2,0,1:T(8,128)(2,1)S(1)}, u32[]{:S(2)}, u32[]{:S(2)}) %all-to-all-start) | async-done | bytes 294944 | tf_op jit(solution)/shard_map/all_to_all | solution.py:83
  107.0 1.2 copy.53
  108.2 29.5 %all-gather.6.cloned.1.call-done = bf16[96,96,128]{2,1,0:T(8,128)(2,1)} async-done(((bf16[12,96,128]{2,1,0:T(8,128)(2,1)}), bf16[96,96,128]{2,1,0:T(8,128)(2,1)}) %all-gather.6.cloned.1.call-update) | async-done | bytes 2359312 | tf_op jit(solution)/shard_map/all_gather | solution.py:88
  137.7 3.5 copy.52
  141.3 3.0 fusion.64
  144.2 1.6 copy.54
  147.7 1.5 add_convert_fusion.1
  150.6 1.2 copy.56
  154.4 1.3 fusion.17
  155.7 44.1 %all-gather.8.cloned.1.call-done = bf16[96,96,128]{2,1,0:T(8,128)(2,1)} async-done(((bf16[12,96,128]{2,1,0:T(8,128)(2,1)}), bf16[96,96,128]{2,1,0:T(8,128)(2,1)}) %all-gather.8.cloned.1.call-update) | async-done | bytes 2359312 | tf_op jit(solution)/shard_map/all_gather | solution.py:106
  199.8 3.5 copy.55
  203.3 3.8 %fusion.66 = f32[128,96,12]{1,2,0:T(8,128)} fusion(bf16[96,96,128]{1,0,2:T(8,128)(2,1)S(1)} %copy.55, bf16[12,96,128]{1,0,2:T(8,128)(2,1)} %copy.59), kind=kOutput, calls=%fused_computation.126 | convolution fusion | flops 28311552 | bytes 3244032 | tf_op jit(solution)/shard_map/kjc,ijc->kic/dot_general | solution.py:109
  207.1 2.4 copy.60
  209.4 2.9 fusion.65
  212.4 1.5 copy.57
  213.9 2.4 bitcast_multiply_fusion.3
  220.8 1.5 fusion.19
  222.3 66.6 %all-reduce.10.cloned.1.call-done = (bf16[128,128]{1,0:T(8,128)(2,1)}, bf16[128,128]{1,0:T(8,128)(2,1)}, bf16[128]{0:T(256)(128)(2,1)}, bf16[128]{0:T(256)(128)(2,1)}) async-done(((bf16[128,128]{1,0:T(8,128)(2,1)}, bf16[128,128]{1,0:T(8,128)(2,1)}, bf16[128]{0:T(256)(128)(2,1)}, bf16[128]{0:T(256)(128)(2,1)}), (bf16[128,128]{1,0:T(8,128)(2,1)}, bf16[128,128]{1,0:T(8,128)(2,1)}, bf16[128]{0:T(256)(128)(2,1)}, ...) | async-done | bytes 66064 | tf_op jit(solution)/shard_map/psum | solution.py:119
  288.9 1.4 convert_element_type.109
  290.3 1.4 convert_element_type.111
  293.9 69.3 %all-reduce.8.cloned.1.call-done = bf16[128,512]{1,0:T(8,128)(2,1)} async-done(((bf16[128,512]{1,0:T(8,128)(2,1)}), bf16[128,512]{1,0:T(8,128)(2,1)}) %all-reduce.8.cloned.1.call-update) | async-done | bytes 131088 | tf_op jit(solution)/shard_map/psum | solution.py:118
  363.2 1.6 convert_element_type.107
  (103 shorter events, 24.0 us)
Async XLA Ops:
  7.2 73.9 %copy-start = (bf16[128,512]{1,0:T(8,128)(2,1)S(1)}, bf16[128,512]{1,0:T(8,128)(2,1)}, u32[]{:S(2)}) copy-start(bf16[128,512]{1,0:T(8,128)(2,1)} %param.26) | copy-start | bytes 393220
  7.2 64.5 %all-gather.4.cloned.1.call-start = ((), (), s32[]{:S(2)}) async-start(), calls=%async_computation.1 | async-start | bytes 2654208 | tf_op jit(solution)/shard_map/all_gather | solution.py:66
  15.9 2.4 copy-start.5
  15.9 2.4 copy-start.23
  15.9 2.4 copy-start.25
  17.0 120.7 %all-gather.6.cloned.1.call-start = ((), (), s32[]{:S(2)}) async-start(), calls=%async_computation.2 | async-start | bytes 2654208 | tf_op jit(solution)/shard_map/all_gather | solution.py:88
  75.2 3.1 copy-start.24
  78.0 1.0 copy-start.6
  78.0 1.2 copy-start.17
  78.0 1.2 copy-start.19
  78.1 2.6 copy-start.22
  79.8 0.8 copy-start.2
  81.1 7.4 %copy-start.14 = (bf16[12,96,128]{2,1,0:T(8,128)(2,1)}, bf16[12,96,128]{2,1,0:T(8,128)(2,1)S(1)}, u32[]{:S(2)}) copy-start(bf16[12,96,128]{2,1,0:T(8,128)(2,1)S(1)} %multiply_convert_fusion.4) | copy-start | bytes 884740
  81.5 1.4 copy-start.1
  82.9 5.5 %copy-start.20 = (bf16[128,128]{1,0:T(8,128)(2,1)S(1)}, bf16[128,128]{1,0:T(8,128)(2,1)}, u32[]{:S(2)}) copy-start(bf16[128,128]{1,0:T(8,128)(2,1)} %param.27) | copy-start | bytes 98308
  84.0 22.9 %copy-start.9 = (bf16[12,96,128]{2,1,0:T(8,128)(2,1)}, bf16[12,96,128]{2,1,0:T(8,128)(2,1)S(1)}, u32[]{:S(2)}) copy-start(bf16[12,96,128]{2,1,0:T(8,128)(2,1)S(1)} %get-tuple-element.22) | copy-start | bytes 884740
  84.9 22.0 %all-to-all-start = ((bf16[12,96,128]{2,0,1:T(8,128)(2,1)}), bf16[12,96,128]{2,0,1:T(8,128)(2,1)S(1)}, u32[]{:S(2)}, u32[]{:S(2)}) async-start(bf16[12,96,128]{2,0,1:T(8,128)(2,1)} %copy.49), calls=%async_computation | async-start | bytes 786432 | tf_op jit(solution)/shard_map/all_to_all | solution.py:83
  88.4 111.4 %all-gather.8.cloned.1.call-start = ((), (), s32[]{:S(2)}) async-start(), calls=%async_computation.3 | async-start | bytes 2654208 | tf_op jit(solution)/shard_map/all_gather | solution.py:106
  141.2 4.9 %copy-start.18 = (bf16[128,128]{1,0:T(8,128)(2,1)S(1)}, bf16[128,128]{1,0:T(8,128)(2,1)}, u32[]{:S(2)}) copy-start(bf16[128,128]{1,0:T(8,128)(2,1)} %param.29) | copy-start | bytes 98308
  141.2 4.9 %copy-start.21 = (f32[128]{0:T(128)S(1)}, f32[128]{0:T(128)}, u32[]{:S(2)}) copy-start(f32[128]{0:T(128)} %param.28) | copy-start | bytes 1540
  144.2 1.9 copy-start.4
  144.2 1.9 copy-start.7
  146.2 3.2 copy-start.11
  146.9 3.7 %copy-start.10 = (bf16[12,96,128]{2,1,0:T(8,128)(2,1)S(1)}, bf16[12,96,128]{2,1,0:T(8,128)(2,1)}, u32[]{:S(2)}) copy-start(bf16[12,96,128]{2,1,0:T(8,128)(2,1)} %copy-done.9) | copy-start | bytes 884740
  147.7 5.9 %copy-start.15 = (bf16[12,96,128]{2,1,0:T(8,128)(2,1)S(1)}, bf16[12,96,128]{2,1,0:T(8,128)(2,1)}, u32[]{:S(2)}) copy-start(bf16[12,96,128]{2,1,0:T(8,128)(2,1)} %copy-done.14) | copy-start | bytes 884740
  149.2 139.7 %all-reduce.10.cloned.1.call-start = ((), (), s32[]{:S(2)}) async-start(), calls=%async_computation.5 | async-start | bytes 133120 | tf_op jit(solution)/shard_map/psum | solution.py:119
  152.8 0.7 copy-start.12
  216.3 1.0 copy-start.16
  217.3 1.1 copy-start.3
  217.3 1.1 copy-start.13
  218.3 2.5 copy-start.8
  220.2 143.0 %all-reduce.8.cloned.1.call-start = ((), (), s32[]{:S(2)}) async-start(), calls=%async_computation.4 | async-start | bytes 262144 | tf_op jit(solution)/shard_map/psum | solution.py:118
Sparse Core Ops, SparseCore 0:
  17.1 54.5 all-gather.3
  84.1 53.5 all-gather.5
  149.3 50.4 all-gather.7
  220.3 68.4 all-reduce.9
  292.6 70.4 all-reduce.7
where the time goes:
time: 372 us; the launch traced here: 371 us
  waiting for transfers between devices  279 us (75%)
  local copies, waits for them, and re-layouts  27.9 us (8%)
  matrix products  23.6 us (6%)
  other arithmetic  22.7 us (6%)
  between operations  14.2 us (4%)
  starting transfers between devices  3.84 us (1%)
    psum x1, waiting for transfers between devices, shards(): lax.psum(grad_proj.astype(jnp.bfloat16), 'dap').astype(jnp.float32)  69.3 us
    psum x1, waiting for transfers between devices, shards(): lax.psum(grad_gate.astype(jnp.bfloat16), 'dap').astype(jnp.float32)  66.6 us
    all_gather x1, waiting for transfers between devices, shards(): lax.all_gather(right_b, 'dap', axis=0, tiled=True)  51.8 us
    all_gather x1, waiting for transfers between devices, shards(): shard_rows = lax.all_gather(grad_x_b, 'dap', axis=0, tiled=True)  44.1 us
    all_gather x1, waiting for transfers between devices, shards(): lax.all_gather(right_ib, 'dap', axis=0, tiled=True)  29.5 us
    all_to_all x1, waiting for transfers between devices, shards(): lax.all_to_all(left_ib, 'dap', split_axis=1, concat_axis=0, tiled=True)  17.3 us
  transfers between devices with their start and end apart: 6, of which 6 were waited for; matrix products, arithmetic and copies ran while one was open for 5% of the time, Pallas kernels for 0%

commit v1 on v0

--- a/solution.py
+++ b/solution.py
@@ -82,11 +82,37 @@
     right_ib = right_in.astype(bf16)
     columns = lax.all_to_all(left_ib, "dap", split_axis=1, concat_axis=0, tiled=True)
     left_block = columns
-    x_in = jnp.einsum(
-        "kic,kjc->ijc",
-        left_block,
-        lax.all_gather(right_ib, "dap", axis=0, tiled=True),
-        preferred_element_type=f32,
+
+    def scan_array_in(mine, a0):
+        aux = lax.axis_size("dap")
+        far_arr = lax.axis_index("dap")
+        x_now, response, r2 = (aux, far_arr, mine.shape[0])
+        series = []
+        for dev in [*range(x_now)]:
+            series.append((dev, (dev + 1) % x_now))
+        store = []
+        for dev in tuple(range(x_now)):
+            store.append((dev, (dev - 1) % x_now))
+        view_out = x_now // 2
+        current_arr = main = mine
+        carry_out = a0(mine, response * r2)
+        for m in [*range(1, view_out + 1)]:
+            current_arr = lax.ppermute(current_arr, axis_name="dap", perm=series)
+            if m < x_now - view_out:
+                main = lax.ppermute(main, axis_name="dap", perm=store)
+                local_now = a0(main, (response + m) % x_now * r2)
+                carry_out = carry_out + local_now
+            carry_out = carry_out + a0(current_arr, (response - m) % x_now * r2)
+        return carry_out
+
+    x_in = scan_array_in(
+        right_ib,
+        lambda shard, offset: jnp.einsum(
+            "kic,kjc->ijc",
+            lax.dynamic_slice_in_dim(left_block, offset, shard.shape[0], axis=0),
+            shard,
+            preferred_element_type=f32,
+        ),
     )
     y_f32, mid_back = jax.vjp(layer_norm, x_in, in_mid_gain)
     y_in = y_f32.astype(bf16)

time: 372 us -> 390 us (1.048)
  local copies, waits for them, and re-layouts: 27.9 us -> 53.6 us
  waiting for transfers between devices: 279 us -> 254 us
  starting transfers between devices: 3.84 us -> 14.7 us
  matrix products: 23.6 us -> 27.8 us
    all_gather x1 -> x0, waiting for transfers between devices: 29.5 us -> none  [shards(): lax.all_gather(right_ib, 'dap', axis=0, tiled=True)]
    ppermute x0 -> x7, waiting for transfers between devices: none -> 18.6 us  [the longest x3 14.2 us: scan_array_in(): main = lax.ppermute(main, axis_name='dap', perm=store)]
    all_to_all x1, waiting for transfers between devices: 17.3 us -> 0.01 us  [shards(): lax.all_to_all(left_ib, 'dap', split_axis=1, concat_axis=0, tiled=True)]
    ppermute x0 -> x7, local copies, waits for them, and re-layouts: none -> 13.6 us  [the longest x4 7.89 us: scan_array_in(): current_arr = lax.ppermute(current_arr, axis_name='dap', perm=series)]
    ppermute x0 -> x7, starting transfers between devices: none -> 11.1 us  [the longest x3 9.21 us: scan_array_in(): main = lax.ppermute(main, axis_name='dap', perm=store)]
    unnamed x52 -> x86, local copies, waits for them, and re-layouts: 3.78 us -> 13.5 us
    dot_general x1 -> x8, local copies, waits for them, and re-layouts: 1.62 us -> 8.69 us  [shards(): jnp.einsum('kic,kjc->ijc', lax.dynamic_slice_in_dim(left_block, offset, s...]
    dot_general x1 -> x8, matrix products: 2.96 us -> 7.93 us  [shards(): jnp.einsum('kic,kjc->ijc', lax.dynamic_slice_in_dim(left_block, offset, s...]
  transfers between devices with their start and end apart: 6 -> 12, of which waited for: 6 -> 7; matrix products, arithmetic and copies ran while one was open for 5% -> 13% of each run, Pallas kernels for 0% -> 0%
where the time goes in v1:
time: 390 us; the launch traced here: 388 us
  waiting for transfers between devices  254 us (65%)
  local copies, waits for them, and re-layouts  53.6 us (14%)
  matrix products  27.8 us (7%)
  other arithmetic  23.8 us (6%)
  starting transfers between devices  14.7 us (4%)
  between operations  14.4 us (4%)
    psum x1, waiting for transfers between devices, shards(): lax.psum(grad_proj.astype(jnp.bfloat16), 'dap').astype(jnp.float32)  69.2 us
    psum x1, waiting for transfers between devices, shards(): lax.psum(grad_gate.astype(jnp.bfloat16), 'dap').astype(jnp.float32)  66.6 us
    all_gather x1, waiting for transfers between devices, shards(): lax.all_gather(right_b, 'dap', axis=0, tiled=True)  51.9 us
    all_gather x1, waiting for transfers between devices, shards(): shard_rows = lax.all_gather(grad_x_b, 'dap', axis=0, tiled=True)  46.9 us
    ppermute x3, waiting for transfers between devices, scan_array_in(): main = lax.ppermute(main, axis_name='dap', perm=store)  14.2 us
    unnamed x86, local copies, waits for them, and re-layouts  13.5 us
    ppermute x3, starting transfers between devices, scan_array_in(): main = lax.ppermute(main, axis_name='dap', perm=store)  9.21 us
    dot_general x8, local copies, waits for them, and re-layouts, shards(): jnp.einsum('kic,kjc->ijc', lax.dynamic_slice_in_dim(left_block, offset, s...  8.69 us
  transfers between devices with their start and end apart: 12, of which 7 were waited for; matrix products, arithmetic and copies ran while one was open for 13% of the time, Pallas kernels for 0%

profile of v1, /device:TPU:0, one launch (start us, length us, event | category | flops | bytes accessed | tf_op | source)
XLA Modules:
  0.0 388.1 jit_solution(10983464398136637770)
XLA Ops:
  10.9 1.6 multiply_reduce_fusion.7
  13.9 1.9 fusion.47
  18.2 1.6 fusion.8
  19.8 51.9 %all-gather.3.cloned.1.call-done = bf16[96,96,128]{2,1,0:T(8,128)(2,1)} async-done(((bf16[12,96,128]{2,1,0:T(8,128)(2,1)}), bf16[96,96,128]{2,1,0:T(8,128)(2,1)}) %all-gather.3.cloned.1.call-update) | async-done | bytes 2359312 | tf_op jit(solution)/shard_map/all_gather | solution.py:66
  71.7 3.5 copy.81
  75.2 2.8 fusion.62
  84.9 3.5 all-to-all-start
  88.4 4.6 %collective-permute-start = (bf16[12,96,128]{2,1,0:T(8,128)(2,1)S(1)}, bf16[12,96,128]{2,1,0:T(8,128)(2,1)}, u32[]{:S(2)}, u32[]{:S(2)}) collective-permute-start(bf16[12,96,128]{2,1,0:T(8,128)(2,1)S(1)} %get-tuple-element.25), channel_id=1, source_target_pairs={{0,28},{4,0},{8,4},{12,8},{16,12},{20,16},{24,20},{28,24},{1,29},{... | collective-permute-start | bytes 884744 | tf_op jit(solution)/shard_map/ppermute | solution.py:102
  93.8 14.2 %collective-permute-done = bf16[12,96,128]{2,1,0:T(8,128)(2,1)} collective-permute-done((bf16[12,96,128]{2,1,0:T(8,128)(2,1)S(1)}, bf16[12,96,128]{2,1,0:T(8,128)(2,1)}, u32[]{:S(2)}, u32[]{:S(2)}) %collective-permute-start) | collective-permute-done | bytes 294944 | tf_op jit(solution)/shard_map/ppermute | solution.py:102
  110.3 2.2 copy.94
  122.1 2.1 copy.122
  124.1 2.0 copy.123
  128.3 2.2 copy.97
  130.5 3.6 collective-permute-start.4
  134.1 1.5 fusion.67
  136.8 2.2 copy.100
  139.0 1.5 fusion.68
  141.6 2.2 copy.103
  150.4 4.0 %collective-permute-done.6 = bf16[12,96,128]{2,1,0:T(8,128)(2,1)} collective-permute-done((bf16[12,96,128]{2,1,0:T(8,128)(2,1)}, bf16[12,96,128]{2,1,0:T(8,128)(2,1)}, u32[]{:S(2)}, u32[]{:S(2)}) %collective-permute-start.6) | collective-permute-done | bytes 294944 | tf_op jit(solution)/shard_map/ppermute | solution.py:100
  154.4 2.2 copy.109
  156.5 1.5 fusion.71
  159.3 2.1 bitcast_reduce_fusion
  169.6 46.9 %all-gather.5.cloned.1.call-done = bf16[96,96,128]{2,1,0:T(8,128)(2,1)} async-done(((bf16[12,96,128]{2,1,0:T(8,128)(2,1)}), bf16[96,96,128]{2,1,0:T(8,128)(2,1)}) %all-gather.5.cloned.1.call-update) | async-done | bytes 2359312 | tf_op jit(solution)/shard_map/all_gather | solution.py:132
  216.5 3.5 copy.111
  220.0 3.8 fusion.73
  223.8 2.4 copy.116
  226.2 3.0 fusion.72
  229.1 1.5 copy.113
  230.7 2.4 bitcast_multiply_fusion.3
  239.0 66.6 %all-reduce.10.cloned.1.call-done = (bf16[128,128]{1,0:T(8,128)(2,1)}, bf16[128,128]{1,0:T(8,128)(2,1)}, bf16[128]{0:T(256)(128)(2,1)}, bf16[128]{0:T(256)(128)(2,1)}) async-done(((bf16[128,128]{1,0:T(8,128)(2,1)}, bf16[128,128]{1,0:T(8,128)(2,1)}, bf16[128]{0:T(256)(128)(2,1)}, bf16[128]{0:T(256)(128)(2,1)}), (bf16[128,128]{1,0:T(8,128)(2,1)}, bf16[128,128]{1,0:T(8,128)(2,1)}, bf16[128]{0:T(256)(128)(2,1)}, ...) | async-done | bytes 66064 | tf_op jit(solution)/shard_map/psum | solution.py:145
  310.7 69.2 %all-reduce.8.cloned.1.call-done = bf16[128,512]{1,0:T(8,128)(2,1)} async-done(((bf16[128,512]{1,0:T(8,128)(2,1)}), bf16[128,512]{1,0:T(8,128)(2,1)}) %all-reduce.8.cloned.1.call-update) | async-done | bytes 131088 | tf_op jit(solution)/shard_map/psum | solution.py:144
  380.0 1.6 convert_element_type.107
  (168 shorter events, 58.2 us)
Async XLA Ops:
  7.2 73.9 %copy-start = (bf16[128,512]{1,0:T(8,128)(2,1)S(1)}, bf16[128,512]{1,0:T(8,128)(2,1)}, u32[]{:S(2)}) copy-start(bf16[128,512]{1,0:T(8,128)(2,1)} %param.26) | copy-start | bytes 393220
  7.2 64.5 %all-gather.3.cloned.1.call-start = ((), (), s32[]{:S(2)}) async-start(), calls=%async_computation.1 | async-start | bytes 2654208 | tf_op jit(solution)/shard_map/all_gather | solution.py:66
  13.9 67.6 %copy-start.25 = (f32[12,96]{1,0:T(8,128)}, f32[12,96]{1,0:T(8,128)S(1)}, u32[]{:S(2)}) copy-start(f32[12,96]{1,0:T(8,128)S(1)} %multiply_convert_fusion.10) | copy-start | bytes 13828
  15.9 2.3 copy-start.4
  75.2 3.1 copy-start.37
  78.1 2.6 copy-start.34
  80.3 2.9 copy-start.27
  81.1 12.4 %copy-start.13 = (bf16[12,96,128]{2,1,0:T(8,128)(2,1)}, bf16[12,96,128]{2,1,0:T(8,128)(2,1)S(1)}, u32[]{:S(2)}) copy-start(bf16[12,96,128]{2,1,0:T(8,128)(2,1)S(1)} %multiply_convert_fusion.4) | copy-start | bytes 884740
  82.9 10.5 %copy-start.30 = (bf16[128,128]{1,0:T(8,128)(2,1)S(1)}, bf16[128,128]{1,0:T(8,128)(2,1)}, u32[]{:S(2)}) copy-start(bf16[128,128]{1,0:T(8,128)(2,1)} %param.27) | copy-start | bytes 98308
  84.9 28.7 %all-to-all-start = ((bf16[12,96,128]{2,0,1:T(8,128)(2,1)}), bf16[12,96,128]{2,0,1:T(8,128)(2,1)S(1)}, u32[]{:S(2)}, u32[]{:S(2)}) async-start(bf16[12,96,128]{2,0,1:T(8,128)(2,1)} %copy.84), calls=%async_computation | async-start | bytes 786432 | tf_op jit(solution)/shard_map/all_to_all | solution.py:83
  88.3 128.2 %all-gather.5.cloned.1.call-start = ((), (), s32[]{:S(2)}) async-start(), calls=%async_computation.2 | async-start | bytes 2654208 | tf_op jit(solution)/shard_map/all_gather | solution.py:132
  88.4 19.6 %collective-permute-start = (bf16[12,96,128]{2,1,0:T(8,128)(2,1)S(1)}, bf16[12,96,128]{2,1,0:T(8,128)(2,1)}, u32[]{:S(2)}, u32[]{:S(2)}) collective-permute-start(bf16[12,96,128]{2,1,0:T(8,128)(2,1)S(1)} %get-tuple-element.25), channel_id=1, source_target_pairs={{0,28},{4,0},{8,4},{12,8},{16,12},{20,16},{24,20},{28,24},{1,29},{... | collective-permute-start | bytes 884744 | tf_op jit(solution)/shard_map/ppermute | solution.py:102
  93.0 17.4 %collective-permute-start.1 = (bf16[12,96,128]{2,1,0:T(8,128)(2,1)S(1)}, bf16[12,96,128]{2,1,0:T(8,128)(2,1)}, u32[]{:S(2)}, u32[]{:S(2)}) collective-permute-start(bf16[12,96,128]{2,1,0:T(8,128)(2,1)S(1)} %get-tuple-element.25), channel_id=1, source_target_pairs={{0,4},{4,8},{8,12},{12,16},{16,20},{20,24},{24,28},{28,0},{1,5},{5... | collective-permute-start | bytes 884744 | tf_op jit(solution)/shard_map/ppermute | solution.py:100
  93.4 27.9 %copy-start.8 = (bf16[12,96,128]{1,0,2:T(8,128)(2,1)}, bf16[12,96,128]{1,0,2:T(8,128)(2,1)S(1)}, u32[]{:S(2)}) copy-start(bf16[12,96,128]{1,0,2:T(8,128)(2,1)S(1)} %copy.88) | copy-start | bytes 884740
  109.4 18.9 %collective-permute-start.2 = (bf16[12,96,128]{2,1,0:T(8,128)(2,1)}, bf16[12,96,128]{2,1,0:T(8,128)(2,1)}, u32[]{:S(2)}, u32[]{:S(2)}) collective-permute-start(bf16[12,96,128]{2,1,0:T(8,128)(2,1)} %collective-permute-done), channel_id=1, source_target_pairs={{0,28},{4,0},{8,4},{12,8},{16,12},{20,16},{24,20},{28,24},{1,29},{... | collective-permute-start | bytes 884744 | tf_op jit(solution)/shard_map/ppermute | solution.py:102
  112.5 21.6 %collective-permute-start.3 = (bf16[12,96,128]{2,1,0:T(8,128)(2,1)}, bf16[12,96,128]{2,1,0:T(8,128)(2,1)}, u32[]{:S(2)}, u32[]{:S(2)}) collective-permute-start(bf16[12,96,128]{2,1,0:T(8,128)(2,1)} %collective-permute-done.1), channel_id=1, source_target_pairs={{0,4},{4,8},{8,12},{12,16},{16,20},{20,24},{24,28},{28,0},{1,5},{5... | collective-permute-start | bytes 884744 | tf_op jit(solution)/shard_map/ppermute | solution.py:100
  121.4 5.2 %copy-start.21 = (bf16[12,12,128]{2,0,1:T(8,128)(2,1)S(1)}, bf16[12,12,128]{2,0,1:T(8,128)(2,1)}, u32[]{:S(2)}) copy-start(bf16[12,12,128]{2,0,1:T(8,128)(2,1)} %get-tuple-element.29) | copy-start | bytes 110596
  121.7 4.4 %copy-start.22 = (bf16[12,12,128]{2,0,1:T(8,128)(2,1)S(1)}, bf16[12,12,128]{2,0,1:T(8,128)(2,1)}, u32[]{:S(2)}) copy-start(bf16[12,12,128]{2,0,1:T(8,128)(2,1)} %get-tuple-element.30) | copy-start | bytes 110596
  121.7 5.4 %copy-start.20 = (bf16[12,12,128]{2,0,1:T(8,128)(2,1)S(1)}, bf16[12,12,128]{2,0,1:T(8,128)(2,1)}, u32[]{:S(2)}) copy-start(bf16[12,12,128]{2,0,1:T(8,128)(2,1)} %get-tuple-element.35) | copy-start | bytes 110596
  130.5 11.1 %collective-permute-start.4 = (bf16[12,96,128]{2,1,0:T(8,128)(2,1)}, bf16[12,96,128]{2,1,0:T(8,128)(2,1)}, u32[]{:S(2)}, u32[]{:S(2)}) collective-permute-start(bf16[12,96,128]{2,1,0:T(8,128)(2,1)} %collective-permute-done.2), channel_id=1, source_target_pairs={{0,28},{4,0},{8,4},{12,8},{16,12},{20,16},{24,20},{28,24},{1,29},{... | collective-permute-start | bytes 884744 | tf_op jit(solution)/shard_map/ppermute | solution.py:102
  134.1 10.1 %collective-permute-start.5 = (bf16[12,96,128]{2,1,0:T(8,128)(2,1)}, bf16[12,96,128]{2,1,0:T(8,128)(2,1)}, u32[]{:S(2)}, u32[]{:S(2)}) collective-permute-start(bf16[12,96,128]{2,1,0:T(8,128)(2,1)} %collective-permute-done.3), channel_id=1, source_target_pairs={{0,4},{4,8},{8,12},{12,16},{16,20},{20,24},{24,28},{28,0},{1,5},{5... | collective-permute-start | bytes 884744 | tf_op jit(solution)/shard_map/ppermute | solution.py:100
  144.2 10.1 %collective-permute-start.6 = (bf16[12,96,128]{2,1,0:T(8,128)(2,1)}, bf16[12,96,128]{2,1,0:T(8,128)(2,1)}, u32[]{:S(2)}, u32[]{:S(2)}) collective-permute-start(bf16[12,96,128]{2,1,0:T(8,128)(2,1)} %collective-permute-done.5), channel_id=1, source_target_pairs={{0,4},{4,8},{8,12},{12,16},{16,20},{20,24},{24,28},{28,0},{1,5},{5... | collective-permute-start | bytes 884744 | tf_op jit(solution)/shard_map/ppermute | solution.py:100
  150.4 8.9 %copy-start.16 = (f32[128,96,12]{0,1,2:T(8,128)S(1)}, f32[128,96,12]{0,1,2:T(8,128)}, u32[]{:S(2)}) copy-start(f32[128,96,12]{0,1,2:T(8,128)} %copy.92) | copy-start | bytes 1769476
  150.4 8.9 %copy-start.17 = (f32[128,96,12]{0,1,2:T(8,128)S(1)}, f32[128,96,12]{0,1,2:T(8,128)}, u32[]{:S(2)}) copy-start(f32[128,96,12]{0,1,2:T(8,128)} %copy.95) | copy-start | bytes 1769476
  161.4 3.0 copy-start.10
  162.1 4.1 %copy-start.24 = (bf16[128,128]{1,0:T(8,128)(2,1)S(1)}, bf16[128,128]{1,0:T(8,128)(2,1)}, u32[]{:S(2)}) copy-start(bf16[128,128]{1,0:T(8,128)(2,1)} %param.29) | copy-start | bytes 98308
  162.2 4.1 %copy-start.33 = (f32[128]{0:T(128)S(1)}, f32[128]{0:T(128)}, u32[]{:S(2)}) copy-start(f32[128]{0:T(128)} %param.28) | copy-start | bytes 1540
  162.9 4.5 %copy-start.14 = (bf16[12,96,128]{2,1,0:T(8,128)(2,1)S(1)}, bf16[12,96,128]{2,1,0:T(8,128)(2,1)}, u32[]{:S(2)}) copy-start(bf16[12,96,128]{2,1,0:T(8,128)(2,1)} %copy-done.13) | copy-start | bytes 884740
  164.4 141.2 %all-reduce.10.cloned.1.call-start = ((), (), s32[]{:S(2)}) async-start(), calls=%async_computation.4 | async-start | bytes 133120 | tf_op jit(solution)/shard_map/psum | solution.py:145
  226.2 4.5 %copy-start.26 = (f32[12,96]{1,0:T(8,128)S(1)}, f32[12,96]{1,0:T(8,128)}, u32[]{:S(2)}) copy-start(f32[12,96]{1,0:T(8,128)} %copy-done.25) | copy-start | bytes 13828
  235.1 2.5 copy-start.7
  237.0 143.0 %all-reduce.8.cloned.1.call-start = ((), (), s32[]{:S(2)}) async-start(), calls=%async_computation.3 | async-start | bytes 262144 | tf_op jit(solution)/shard_map/psum | solution.py:144
  (19 other events, 26.2 us)
Sparse Core Ops, SparseCore 0:
  17.1 54.5 all-gather.2
  164.6 51.8 all-gather.4
  237.1 68.4 all-reduce.9
  309.4 70.4 all-reduce.7
